TPU v7x, 32 devices: a whole 2x2x4 slice. The times are simulated.
32 devices in a mesh: grp: 4 (over y, x), tp: 8 (over z, core).
Axes of the slice: x: 2, y: 2, z: 4, core: 2. Of those that a mesh axis runs over, the one named last changes fastest.
Arguments:
- key_cache: bfloat16 [4, 8, 768, 512], P('grp', 'tp'), may hold values from -6 to 6
- value_cache: bfloat16 [4, 8, 768, 512], P('grp', 'tp'), may hold values from -12 to 12
- lengths: int32 [4, 8], P('grp', 'tp'), may hold values from 256 to 768, as said below
- queries: bfloat16 [4, 1, 8, 8192], P('grp', None, 'tp'), may hold values from -12 to 12
- new_keys: bfloat16 [4, 1, 8, 512], P('grp', None, 'tp'), may hold values from -18 to 18
- new_values: bfloat16 [4, 1, 8, 512], P('grp', None, 'tp'), may hold values from -12 to 12
- residual: bfloat16 [4, 1, 8, 8192], P('grp', None, 'tp'), may hold values from -4 to 4
- norm_gain: float32 [8192], replicated, may hold values from 0.25 to 1.75
- gate_weight: bfloat16 [4, 13312, 8192], P('grp', 'tp'), may hold values from -0.0625 to 0.0625
- up_weight: bfloat16 [4, 13312, 8192], P('grp', 'tp'), may hold values from -0.0625 to 0.0625
- down_weight: bfloat16 [4, 13312, 8192], P('grp', 'tp'), may hold values from -0.0390625 to 0.0390625
Outputs:
- mixed: bfloat16 [4, 1, 8, 8192], P('grp', None, 'tp')
Inputs may be any that keep to these rules, and one draw needn't show every extreme that they name: `lengths`: some row has exactly 768 valid positions.
All inputs are finite; a program needn't handle non-finite values.
Results may differ from a plain program's by a relative error of at most 0.005.
Values may be sent and summed in bfloat16 or wider, within the bound.
A program may use at most 128 MiB of HBM per device.

v0:
```python
import jax
import jax.numpy as jnp
from jax import lax
from jax.sharding import PartitionSpec as P

HEADS = 64
HD = 128
KVH = 4


masked_score = -1e30


def feed_rows(normed_rows, gate_weight, up_weight, down_weight):
    numbers = (((1,), (1,)), ((), ()))
    gate_part = lax.dot_general(
        normed_rows, gate_weight[0], numbers, preferred_element_type=jnp.float32
    )
    up_part = lax.dot_general(
        normed_rows, up_weight[0], numbers, preferred_element_type=jnp.float32
    )
    product = (jax.nn.silu(gate_part) * up_part).astype(jnp.bfloat16)
    return jnp.dot(product, down_weight[0], preferred_element_type=jnp.float32)


def local(
    key_cache,
    value_cache,
    lengths,
    queries,
    new_keys,
    new_values,
    residual,
    norm_gain,
    gate_weight,
    up_weight,
    down_weight,
):
    groups = lax.axis_size("grp")
    members = lax.axis_size("tp")
    serving = lax.axis_index("grp") < groups // 2
    step_count = queries.shape[1]
    own_rows = queries.shape[2]
    model_width = queries.shape[3]
    head_share = HEADS // KVH
    slot_count = key_cache.shape[2]
    score_scale = HD ** (-0.5)
    own_heads = queries[0].reshape(step_count, own_rows, KVH, head_share, HD)
    cache_keys = key_cache[0].reshape(own_rows, slot_count, KVH, HD)
    cache_values = value_cache[0].reshape(own_rows, slot_count, KVH, HD)
    positions = jnp.arange(slot_count)
    usable = positions[None, :] < lengths[0][:, None]
    usable_mask = usable[None, :, None, None, :]
    cache_scores = (
        jnp.einsum("srjgd,rpjd->srjgp", own_heads, cache_keys, preferred_element_type=jnp.float32)
        * score_scale
    )
    cache_scores = jnp.where(usable_mask, cache_scores, masked_score)
    fresh_keys = new_keys[0].reshape(step_count, own_rows, KVH, HD)
    fresh_values = new_values[0].reshape(step_count, own_rows, KVH, HD)
    fresh_scores = (
        jnp.einsum("srjgd,trjd->srjgt", own_heads, fresh_keys, preferred_element_type=jnp.float32)
        * score_scale
    )
    causal = jnp.arange(step_count)[:, None] >= jnp.arange(step_count)[None, :]
    causal_mask = causal[:, None, None, None, :]
    fresh_scores = jnp.where(causal_mask, fresh_scores, masked_score)
    ceiling = jnp.maximum(jnp.max(cache_scores, axis=-1), jnp.max(fresh_scores, axis=-1))
    cache_exp = jnp.where(usable_mask, jnp.exp(cache_scores - ceiling[..., None]), 0.0)
    fresh_exp = jnp.where(causal_mask, jnp.exp(fresh_scores - ceiling[..., None]), 0.0)
    denominator = jnp.sum(cache_exp, axis=-1) + jnp.sum(fresh_exp, axis=-1)
    cache_weighted = jnp.einsum(
        "srjgp,rpjd->srjgd",
        cache_exp.astype(jnp.bfloat16),
        cache_values,
        preferred_element_type=jnp.float32,
    )
    fresh_weighted = jnp.einsum(
        "srjgt,trjd->srjgd",
        fresh_exp.astype(jnp.bfloat16),
        fresh_values,
        preferred_element_type=jnp.float32,
    )
    attended = (cache_weighted + fresh_weighted) / denominator[..., None]
    attended = attended.reshape(step_count, own_rows, model_width)
    hidden = residual[0].astype(jnp.float32) + attended
    spread_sq = jnp.mean(hidden * hidden, axis=-1, keepdims=True)
    normed = (hidden * lax.rsqrt(spread_sq + 1e-05) * norm_gain).astype(jnp.bfloat16)
    block_rows = step_count * own_rows
    flat_rows = normed.reshape(block_rows, model_width)
    ffn_first = groups // 2
    group_block = lax.all_gather(flat_rows, "tp", axis=0, tiled=True).reshape(
        members, block_rows, model_width
    )
    all_rows = lax.all_gather(group_block, "grp", axis=1, tiled=True)
    real_rows = all_rows[:, : ffn_first * block_rows].reshape(
        members * ffn_first * block_rows, model_width
    )
    within = lax.psum_scatter(
        lax.cond(
            serving,
            lambda operand: jnp.zeros(
                (ffn_first * block_rows * lax.axis_size("tp"), model_width), jnp.float32
            ),
            lambda operand: feed_rows(operand, gate_weight, up_weight, down_weight),
            real_rows,
        ),
        "tp",
        scatter_dimension=0,
        tiled=True,
    )
    padded = jnp.concatenate(
        [within, jnp.zeros(((groups - ffn_first) * block_rows, model_width), jnp.float32)], 0
    )
    summed = lax.psum_scatter(padded, "grp", scatter_dimension=0, tiled=True)
    mixed = (hidden + summed.reshape(step_count, own_rows, model_width)).astype(jnp.bfloat16)
    mixed = jnp.where(serving, mixed, jnp.zeros_like(mixed))
    return mixed[None]


def solution(mesh):
    return jax.shard_map(
        local,
        mesh=mesh,
        in_specs=(
            P("grp", "tp", None, None),
            P("grp", "tp", None, None),
            P("grp", "tp"),
            P("grp", None, "tp", None),
            P("grp", None, "tp", None),
            P("grp", None, "tp", None),
            P("grp", None, "tp", None),
            P(),
            P("grp", "tp", None),
            P("grp", "tp", None),
            P("grp", "tp", None),
        ),
        out_specs=P("grp", None, "tp", None),
        check_vma=False,
    )
```

profile of v0, /device:TPU:0, one launch (start us, length us, event | category | flops | bytes accessed | tf_op | source)
XLA Modules:
  0.0 188.5 jit_solution(14599634890557836540)
XLA Ops:
  6.5 0.0 copy-start
  6.5 0.0 all-reduce.6.cloned.1.call-start
  7.2 1.8 reshape.145
  9.0 0.0 copy-done
  9.0 0.1 reduce.4
  9.1 0.8 fusion.38
  9.9 0.4 fusion.42
  10.3 0.2 fusion.28
  10.5 0.8 convert_element_type.47
  11.3 1.8 reshape.149
  13.1 0.7 convert.12
  13.8 0.9 fusion.37
  15.3 0.8 multiply_convert_fusion
  16.1 15.7 %all-gather = bf16[65536]{0:T(1024)(128)(2,1)S(1)} all-gather(bf16[8192]{0:T(1024)(128)(2,1)S(1)} %multiply_convert_fusion), channel_id=2, replica_groups=mesh['grp'=4,'tp'=8] {'tp'}, dimensions={0}, use_global_device_ids=true | all-gather | bytes 147456 | tf_op jit(solution)/shard_map/all_gather | solution.py:92
  31.8 0.1 reshape.161
  31.9 10.3 %all-gather.1 = bf16[8,32768]{1,0:T(8,128)(2,1)S(1)} all-gather(bf16[8,8192]{1,0:T(8,128)(2,1)S(1)} %reshape.161), channel_id=3, replica_groups=mesh['grp'=4,'tp'=8] {'grp'}, dimensions={1}, use_global_device_ids=true | all-gather | bytes 655360 | tf_op jit(solution)/shard_map/all_gather | solution.py:95
  42.2 0.4 reshape.162
  42.6 0.0 copy-start.5
  42.6 0.0 copy-start.4
  42.6 0.0 copy-start.3
  42.7 0.1 conditional.1
  42.7 0.0 copy-start.2
  42.7 0.0 copy-start.1
  42.7 0.8 copy-done.2
  43.5 0.0 all-reduce.6.cloned.1.call-update
  43.6 0.0 all-reduce.8.cloned.1.call-start
  43.6 0.0 copy-done.5
  43.6 0.6 dynamic-slice
  44.9 90.4 %all-reduce.6.cloned.1.call-done = f32[16,8192]{1,0:T(8,128)} async-done(((f32[16,8192]{1,0:T(8,128)}), f32[16,8192]{1,0:T(8,128)}) %all-reduce.6.cloned.1.call-update) | async-done | bytes 524304
  135.3 1.0 constant_dynamic-slice_fusion
  136.3 0.7 concatenate.3
  137.0 0.0 all-reduce.8.cloned.1.call-update
  137.0 0.0 copy-done.4
  137.0 0.6 dynamic-slice.2
  137.6 41.8 %all-reduce.8.cloned.1.call-done = f32[4,8192]{1,0:T(4,128)} async-done(((f32[4,8192]{1,0:T(4,128)}), f32[4,8192]{1,0:T(4,128)}) %all-reduce.8.cloned.1.call-update) | async-done | bytes 131088
  179.5 0.0 copy-done.3
  179.5 2.2 %broadcast_select_fusion = bf16[1,1,1,8192]{3,2,1,0:T(2,128)(2,1)} fusion(pred[]{:T(512)S(6)} %lt.19, f32[4,8192]{1,0:T(4,128)} %all-reduce.8.cloned.1.call-done, u32[]{:T(128)} %bitcast.23, f32[1,1,1,8192]{3,2,1,0:T(1,128)S(1)} %bitcast.74, bf16[1,1,1,8192]{3,2,1,0:T(2,128)(2,1)S(1)} %copy-done.3), kind=kLoop, calls=%fused_computation.31 | loop fusion | flops 40960 | bytes 98309 | tf_op jit(solution)/shard_map/jit(_where)/select_n | solution.py:117
  181.7 0.0 copy-done.1
  (4 shorter events, 0.1 us)
Async XLA Ops:
  6.5 2.4 %copy-start = (bf16[1,1,1,8192]{3,2,1,0:T(2,128)(2,1)S(1)}, bf16[1,1,1,8192]{3,2,1,0:T(2,128)(2,1)}, u32[]{:S(2)}) copy-start(bf16[1,1,1,8192]{3,2,1,0:T(2,128)(2,1)} %param.16) | copy-start | bytes 49156
  6.5 128.8 %all-reduce.6.cloned.1.call-start = ((), (), s32[]{:S(2)}) async-start(), calls=%async_computation | async-start | bytes 1048576
  42.6 1.0 copy-start.5
  42.6 94.4 %copy-start.4 = (u32[32]{0:T(128)S(1)}, u32[32]{0:T(128)}, u32[]{:S(2)}) copy-start(u32[32]{0:T(128)} %constant.51) | copy-start | bytes 388
  42.6 136.8 %copy-start.3 = (bf16[1,1,1,8192]{3,2,1,0:T(2,128)(2,1)S(1)}, bf16[1,1,1,8192]{3,2,1,0:T(2,128)(2,1)}, u32[]{:S(2)}) copy-start(bf16[1,1,1,8192]{3,2,1,0:T(2,128)(2,1)} %param.19) | copy-start | bytes 49156
  42.7 0.8 copy-start.2
  42.7 139.0 %copy-start.1 = (bf16[1,1,1,8192]{3,2,1,0:T(2,128)(2,1)S(1)}, bf16[1,1,1,8192]{3,2,1,0:T(2,128)(2,1)}, u32[]{:S(2)}) copy-start(bf16[1,1,1,8192]{3,2,1,0:T(2,128)(2,1)} %param.16) | copy-start | bytes 49156
  43.6 135.9 %all-reduce.8.cloned.1.call-start = ((), (), s32[]{:S(2)}) async-start(), calls=%async_computation.1 | async-start | bytes 262144
Sparse Core Ops, SparseCore 0:
  43.7 91.5 all-reduce.5
  138.2 41.2 all-reduce.7
where the time goes:
time: 189 us
  waiting for transfers between devices  132 us (70%)
  blocking collectives  26 us (14%)
  between operations  15.5 us (8%)
  local copies, waits for them, and re-layouts  7.69 us (4%)
  other arithmetic  4.78 us (3%)
  matrix products  2.09 us (1%)
    unnamed x4, waiting for transfers between devices  132 us
    all_gather x1, blocking collectives, local(): lax.all_gather(flat_rows, 'tp', axis=0, tiled=True)  15.7 us
    all_gather x1, blocking collectives, local(): all_rows = lax.all_gather(group_block, 'grp', axis=1, tiled=True)  10.3 us
  transfers between devices with their start and end apart: 2, of which 2 were waited for; matrix products, arithmetic and copies ran while one was open for 1% of the time, Pallas kernels for 0%

commit v1 on v0

v1 whole, which is shorter than its diff:
```python
import functools

import jax
import jax.numpy as jnp
from jax import lax
from jax.experimental import pallas as pl
from jax.experimental.pallas import tpu as pltpu
from jax.sharding import PartitionSpec as P

HEADS = 64
HD = 128
KVH = 4
SHARE = HEADS // KVH

masked_score = -1e30
MESH_ID = pl.DeviceIdType.MESH
VMEM_BYTES = 66_000_000


def kernel(
    plan,
    lengths,
    queries,
    fresh_keys,
    fresh_values,
    residual,
    gain,
    key_hbm,
    value_hbm,
    gate_hbm,
    up_hbm,
    down_hbm,
    out,
    keys,
    values,
    hidden,
    normed,
    box,
    wide,
    rows,
    act,
    part,
    slots,
    down_slots,
    cache_sem,
    slot_sem,
    down_sem,
    send_sem,
    recv_sem,
):
    (half, members, chunk, chunks, ring, down_cols, down_chunks, down_ring, batch) = plan
    peers = half * members
    blocks = HEADS
    group = lax.axis_index("grp")
    member = lax.axis_index("tp")
    serving = group < half
    mine = lax.rem(group, half) * members + member
    other = jnp.where(serving, half, 0)
    barrier = pltpu.get_barrier_semaphore()

    def peer_id(i):
        return {"grp": other + i // members, "tp": lax.rem(i, members)}

    def slot_copies(i, s):
        start = pl.multiple_of(i * chunk, chunk)
        return (
            pltpu.make_async_copy(
                gate_hbm.at[0, pl.ds(start, chunk), :], slots.at[s, 0], slot_sem.at[s]
            ),
            pltpu.make_async_copy(
                up_hbm.at[0, pl.ds(start, chunk), :], slots.at[s, 1], slot_sem.at[s]
            ),
        )

    def down_copy(c, s):
        start = pl.multiple_of(c * down_cols, down_cols)
        return pltpu.make_async_copy(
            down_hbm.at[0, :, pl.ds(start, down_cols)], down_slots.at[s], down_sem.at[s]
        )

    key_copy = pltpu.make_async_copy(key_hbm.at[0, 0], keys, cache_sem.at[0])
    value_copy = pltpu.make_async_copy(value_hbm.at[0, 0], values, cache_sem.at[1])

    @pl.when(serving)
    def _():
        key_copy.start()
        value_copy.start()

    @pl.when(jnp.logical_not(serving))
    def _():
        for i in range(min(ring, chunks)):
            for copy in slot_copies(i, i):
                copy.start()

    @pl.loop(0, peers)
    def _(i):
        pl.semaphore_signal(barrier, inc=1, device_id=peer_id(i), device_id_type=MESH_ID)

    @pl.when(serving)
    def _():
        slot_count = keys.shape[0]
        scale = HD ** (-0.5)
        usable = lax.broadcasted_iota(jnp.int32, (SHARE, slot_count), 1) < lengths[0, 0]
        key_copy.wait()
        value_copy.wait()
        spread = jnp.zeros((1, 1), jnp.float32)
        for j in range(KVH):
            head = slice(j * SHARE, (j + 1) * SHARE)
            lanes = slice(j * HD, (j + 1) * HD)
            own = queries[head, :]
            scores = (
                lax.dot_general(
                    own, keys[:, lanes], (((1,), (1,)), ((), ())),
                    preferred_element_type=jnp.float32,
                )
                * scale
            )
            scores = jnp.where(usable, scores, masked_score)
            fresh = (
                jnp.sum(
                    own.astype(jnp.float32) * fresh_keys[j : j + 1, :].astype(jnp.float32),
                    axis=-1, keepdims=True,
                )
                * scale
            )
            ceiling = jnp.maximum(jnp.max(scores, axis=-1, keepdims=True), fresh)
            expo = jnp.where(usable, jnp.exp(scores - ceiling), 0.0)
            fresh_expo = jnp.exp(fresh - ceiling)
            denominator = jnp.sum(expo, axis=-1, keepdims=True) + fresh_expo
            total = jnp.dot(
                expo.astype(jnp.bfloat16), values[:, lanes], preferred_element_type=jnp.float32
            )
            total = total + fresh_expo.astype(jnp.bfloat16).astype(jnp.float32) * fresh_values[
                j : j + 1, :
            ].astype(jnp.float32)
            row = residual[head, :].astype(jnp.float32) + total / denominator
            hidden[head, :] = row
            squares = jnp.sum(row * row, axis=-1, keepdims=True)
            spread = spread + jnp.sum(squares, axis=0, keepdims=True)
        factor = lax.rsqrt(spread / (HEADS * HD) + 1e-05)
        normed[...] = (hidden[...] * factor * gain[...]).astype(jnp.bfloat16)
        pl.semaphore_wait(barrier, peers)

        @pl.loop(0, peers)
        def _(i):
            to = lax.rem(mine + i, peers)
            pltpu.make_async_remote_copy(
                src_ref=normed,
                dst_ref=box.at[mine],
                send_sem=send_sem,
                recv_sem=recv_sem,
                device_id=peer_id(to),
                device_id_type=MESH_ID,
            ).start()

        pltpu.make_async_copy(box, box, send_sem).wait()
        pltpu.make_async_copy(box, box, recv_sem).wait()

        for b in range(0, blocks, batch):
            band = slice(b, b + batch)
            total = hidden[band, :]
            feed = lax.fori_loop(
                0,
                peers,
                lambda f, so_far: so_far + box[f, band, :].astype(jnp.float32),
                jnp.zeros_like(total),
            )
            out[band, :] = (total + feed).astype(jnp.bfloat16)

    @pl.when(jnp.logical_not(serving))
    def _():
        out[...] = jnp.zeros_like(out)
        pl.semaphore_wait(barrier, peers)
        pltpu.make_async_copy(box, box, recv_sem).wait()
        for c in range(min(down_ring, down_chunks)):
            down_copy(c, c).start()

        @pl.loop(0, peers)
        def _(r):
            wide[pl.ds(pl.multiple_of(r * blocks, blocks), blocks), :] = box[r].astype(jnp.float32)

        for h in range(blocks):
            rows[:, h * HD : (h + 1) * HD] = wide[pl.ds(h, peers, stride=blocks), :].astype(
                jnp.bfloat16
            )

        numbers = (((1,), (1,)), ((), ()))

        def product(weights):
            mid = weights.shape[1] // 2
            return lax.dot_general(
                rows[:, :mid], weights[:, :mid], numbers, preferred_element_type=jnp.float32
            ) + lax.dot_general(
                rows[:, mid:], weights[:, mid:], numbers, preferred_element_type=jnp.float32
            )

        def hidden_units(i, s):
            pltpu.make_async_copy(slots.at[s], slots.at[s], slot_sem.at[s]).wait()
            gate = product(slots[s, 0])
            up = product(slots[s, 1])
            return (gate / (1.0 + jnp.exp(-gate)) * up).astype(jnp.bfloat16)

        if chunks == 1:
            act[...] = hidden_units(0, 0)
        else:

            @pl.loop(0, chunks)
            def _(i):
                s = lax.rem(i, ring)
                act[:, pl.ds(pl.multiple_of(i * chunk, chunk), chunk)] = hidden_units(i, s)

                @pl.when(i + ring < chunks)
                def _():
                    for copy in slot_copies(i + ring, s):
                        copy.start()

        per_chunk = down_cols // HD
        per_send = batch // per_chunk

        @pl.loop(0, down_chunks // per_send)
        def _(g):
            base = pl.multiple_of(g * batch, batch)
            for k in range(per_send):
                c = g * per_send + k
                s = lax.rem(c, down_ring)
                pltpu.make_async_copy(down_slots.at[s], down_slots.at[s], down_sem.at[s]).wait()
                feed = jnp.dot(act[...], down_slots[s], preferred_element_type=jnp.float32)

                @pl.when(c + down_ring < down_chunks)
                def _():
                    down_copy(c + down_ring, s).start()

                for h in range(per_chunk):
                    wide[pl.ds(base + k * per_chunk + h, peers, stride=blocks), :] = feed[
                        :, h * HD : (h + 1) * HD
                    ]

            @pl.loop(0, peers)
            def _(r):
                start = pl.multiple_of(r * blocks + base, batch)
                part[r, pl.ds(base, batch), :] = wide[pl.ds(start, batch), :].astype(jnp.bfloat16)

            @pl.loop(0, peers)
            def _(i):
                to = lax.rem(mine + i, peers)
                pltpu.make_async_remote_copy(
                    src_ref=part.at[to, pl.ds(base, batch), :],
                    dst_ref=box.at[mine, pl.ds(base, batch), :],
                    send_sem=send_sem,
                    recv_sem=recv_sem,
                    device_id=peer_id(to),
                    device_id_type=MESH_ID,
                ).start()

        pltpu.make_async_copy(part, part, send_sem).wait()


def local(
    key_cache,
    value_cache,
    lengths,
    queries,
    new_keys,
    new_values,
    residual,
    norm_gain,
    gate_weight,
    up_weight,
    down_weight,
):
    groups = lax.axis_size("grp")
    members = lax.axis_size("tp")
    half = groups // 2
    peers = half * members
    width = queries.shape[3]
    slot_count = key_cache.shape[2]
    units = gate_weight.shape[1]
    chunk = HD if units % HD == 0 else units
    chunks = units // chunk
    slot_bytes = 4 * chunk * width
    ring = max(1, min(chunks, 42_000_000 // slot_bytes))
    down_cols = 512
    down_chunks = width // down_cols
    down_ring = min(down_chunks, max(1, 14_000_000 // (2 * units * down_cols)))
    batch = 16
    plan = (half, members, chunk, chunks, ring, down_cols, down_chunks, down_ring, batch)
    vmem = pl.BlockSpec(memory_space=pltpu.VMEM)
    any_space = pl.BlockSpec(memory_space=pl.ANY)
    bf16 = jnp.bfloat16
    f32 = jnp.float32
    mixed = pl.pallas_call(
        functools.partial(kernel, plan),
        out_shape=jax.ShapeDtypeStruct((HEADS, HD), bf16),
        in_specs=[pl.BlockSpec(memory_space=pltpu.SMEM)] + [vmem] * 5 + [any_space] * 5,
        out_specs=vmem,
        scratch_shapes=[
            pltpu.VMEM((slot_count, KVH * HD), bf16),
            pltpu.VMEM((slot_count, KVH * HD), bf16),
            pltpu.VMEM((HEADS, HD), f32),
            pltpu.VMEM((HEADS, HD), bf16),
            pltpu.VMEM((peers, HEADS, HD), bf16),
            pltpu.VMEM((peers * HEADS, HD), f32),
            pltpu.VMEM((peers, width), bf16),
            pltpu.VMEM((peers, units), bf16),
            pltpu.VMEM((peers, HEADS, HD), bf16),
            pltpu.VMEM((ring, 2, chunk, width), bf16),
            pltpu.VMEM((down_ring, units, down_cols), bf16),
            pltpu.SemaphoreType.DMA((2,)),
            pltpu.SemaphoreType.DMA((ring,)),
            pltpu.SemaphoreType.DMA((down_ring,)),
            pltpu.SemaphoreType.DMA,
            pltpu.SemaphoreType.DMA,
        ],
        compiler_params=pltpu.CompilerParams(
            collective_id=0, has_side_effects=True, vmem_limit_bytes=VMEM_BYTES
        ),
    )(
        lengths,
        queries.reshape(HEADS, HD),
        new_keys.reshape(KVH, HD),
        new_values.reshape(KVH, HD),
        residual.reshape(HEADS, HD),
        norm_gain.reshape(HEADS, HD),
        key_cache,
        value_cache,
        gate_weight,
        up_weight,
        down_weight,
    )
    return mixed.reshape(1, 1, 1, width)


def solution(mesh):
    return jax.shard_map(
        local,
        mesh=mesh,
        in_specs=(
            P("grp", "tp", None, None),
            P("grp", "tp", None, None),
            P("grp", "tp"),
            P("grp", None, "tp", None),
            P("grp", None, "tp", None),
            P("grp", None, "tp", None),
            P("grp", None, "tp", None),
            P(),
            P("grp", "tp", None),
            P("grp", "tp", None),
            P("grp", "tp", None),
        ),
        out_specs=P("grp", None, "tp", None),
        check_vma=False,
    )
```

time: 189 us -> 53 us (0.28)
  waiting for transfers between devices: 132 us -> 0 us
  Pallas kernels: 0 us -> 45.1 us
  blocking collectives: 26 us -> 0 us
  between operations: 15.5 us -> 0.66 us
  local copies, waits for them, and re-layouts: 7.69 us -> 1.34 us
  matrix products: 2.09 us -> 0 us
    unnamed x4 -> x0, waiting for transfers between devices: 132 us -> none
    pallas_call x0 -> x1, Pallas kernels: none -> 45.1 us  [local(): pl.pallas_call(functools.partial(kernel, plan), out_shape=jax.ShapeDtypeS...]
    all_gather x2 -> x0, blocking collectives: 26 us -> none  [the longest x1 15.7 us: local(): lax.all_gather(flat_rows, 'tp', axis=0, tiled=True)]
    unnamed x1 -> x4, other arithmetic: 0.09 us -> 5.43 us
    another operation x3 -> x0, local copies, waits for them, and re-layouts: 3.54 us -> none
    unnamed x15 -> x0, local copies, waits for them, and re-layouts: 3.03 us -> none
    select_n x1 -> x0, other arithmetic: 2.21 us -> none  [local(): mixed = jnp.where(serving, mixed, jnp.zeros_like(mixed))]
    dot_general x3 -> x0, matrix products: 2.09 us -> none  [the longest x1 0.89 us: local(): jnp.einsum('srjgp,rpjd->srjgd', cache_exp.astype(jnp.bfloat16), cache_val...]
  transfers between devices with their start and end apart: 2 -> 0, of which waited for: 2 -> 0; matrix products, arithmetic and copies ran while one was open for 1% -> 0% of each run, Pallas kernels for 0% -> 0%
where the time goes in v1:
time: 53 us; the launch traced here: 52.5 us
  Pallas kernels  45.1 us (85%)
  other arithmetic  5.43 us (10%)
  local copies, waits for them, and re-layouts  1.34 us (3%)
  between operations  0.66 us (1%)
    pallas_call x1, Pallas kernels, local(): pl.pallas_call(functools.partial(kernel, plan), out_shape=jax.ShapeDtypeS...  45.1 us
    unnamed x4, other arithmetic  5.43 us
    reshape x1, local copies, waits for them, and re-layouts, local(): return mixed.reshape(1, 1, 1, width)  1.34 us

profile of v1, /device:TPU:0, one launch (start us, length us, event | category | flops | bytes accessed | tf_op | source)
XLA Modules:
  0.0 52.5 jit_solution(6571214720821019163)
XLA Ops:
  0.7 1.3 %reduce.1 = bf16[512]{0:T(512)(128)(2,1)} reduce(bf16[1,1,1,512]{3,2,1,0:T(2,128)(2,1)} %param.15, bf16[]{:T(256)} %constant.10), dimensions={0,1,2}, to_apply=%param.15.reduce_sub_computation | reduce | bytes 2050 | tf_op args[4]
  1.9 1.3 %reduce.2 = bf16[512]{0:T(512)(128)(2,1)} reduce(bf16[1,1,1,512]{3,2,1,0:T(2,128)(2,1)} %param.16, bf16[]{:T(256)} %constant.10), dimensions={0,1,2}, to_apply=%param.16.reduce_sub_computation | reduce | bytes 2050 | tf_op args[5]
  3.2 1.5 %reduce = bf16[8192]{0:T(1024)(128)(2,1)} reduce(bf16[1,1,1,8192]{3,2,1,0:T(2,128)(2,1)} %param.14, bf16[]{:T(256)} %constant.10), dimensions={0,1,2}, to_apply=%param.14.reduce_sub_computation | reduce | bytes 32770 | tf_op args[3]
  4.6 1.4 %reduce.3 = bf16[8192]{0:T(1024)(128)(2,1)} reduce(bf16[1,1,1,8192]{3,2,1,0:T(2,128)(2,1)} %param.17, bf16[]{:T(256)} %constant.10), dimensions={0,1,2}, to_apply=%param.17.reduce_sub_computation | reduce | bytes 32770 | tf_op args[6]
  6.1 45.1 %shard_map.109 = bf16[64,128]{1,0:T(8,128)(2,1)} custom-call(s32[1,1]{1,0:T(1,128)S(6)} %copy.12.lengths, bf16[64,128]{1,0:T(8,128)(2,1)} %bitcast.5, bf16[4,128]{1,0:T(4,128)(2,1)} %bitcast.8, bf16[4,128]{1,0:T(4,128)(2,1)} %bitcast.9, bf16[64,128]{1,0:T(8,128)(2,1)} %bitcast.6, f32[64,128]{1,0:T(8,128)} %bitcast.7, bf16[1,1,768,512]{3,2,1,0:T(8,128)(2,1)} %key_hbm.1, ...), custom_call_target="tpu_custom_call" | custom-call | tf_op jit(solution)/shard_map/pallas_call | solution.py:291
  51.2 1.3 %reshape.23 = bf16[1,1,1,8192]{3,2,1,0:T(2,128)(2,1)} reshape(bf16[64,128]{1,0:T(8,128)(2,1)} %shard_map.109) | data formatting | bytes 32768 | tf_op jit(solution)/shard_map/reshape | solution.py:330
